TPU v7x, 32 devices: a whole 2x2x4 slice. The times are simulated.
32 devices in a mesh: dp: 16 (over z, y, core), tensor: 2 (over x).
Axes of the slice: x: 2, y: 2, z: 4, core: 2. Of those that a mesh axis runs over, the one named last changes fastest.
Arguments:
- hidden_in: bfloat16 [8192, 1536], P('dp'), may hold values from -6 to 6
- norm_gain: float32 [1536], replicated, may hold values from 0.1 to 1.9
- weight_gate: bfloat16 [1536, 3072], P(None, 'tensor'), may hold values from -0.15625 to 0.15625
- weight_value: bfloat16 [1536, 3072], P(None, 'tensor'), may hold values from -0.15625 to 0.15625
- weight_step: bfloat16 [1536, 48], P(None, 'tensor'), may hold values from -0.15625 to 0.15625
- weight_scan: bfloat16 [1536, 256], replicated, may hold values from -0.15625 to 0.15625
- conv_value: float32 [4, 3072], P(None, 'tensor'), may hold values from -3 to 3
- conv_value_bias: float32 [3072], P('tensor'), may hold values from -0.5 to 0.5
- conv_scan: float32 [4, 256], replicated, may hold values from -3 to 3
- conv_scan_bias: float32 [256], replicated, may hold values from -0.5 to 0.5
- step_bias: float32 [48], P('tensor'), may hold values from -6.9 to -2.3
- decay_log: float32 [48], P('tensor'), may hold values from 0 to 2.77
- skip_gain: float32 [48], P('tensor'), may hold values from 0.5 to 1.5
- gate_gain: float32 [3072], P('tensor'), may hold values from 0.1 to 1.9
- weight_out: bfloat16 [3072, 1536], P('tensor'), may hold values from -0.15625 to 0.15625
- cotangent: bfloat16 [8192, 1536], P('dp'), may hold values from -6 to 6
Outputs:
- block_out: float32 [8192, 1536], P('dp', 'tensor')
- grad_in: float32 [8192, 1536], P('dp', 'tensor')
- grad_norm_gain: float32 [1536], P('tensor')
- grad_weight_gate: float32 [1536, 3072], P(None, 'tensor')
- grad_weight_value: float32 [1536, 3072], P(None, 'tensor')
- grad_weight_step: float32 [1536, 48], P(None, 'tensor')
- grad_weight_scan: float32 [1536, 256], replicated
- grad_conv_value: float32 [4, 3072], P(None, 'tensor')
- grad_conv_value_bias: float32 [3072], P('tensor')
- grad_conv_scan: float32 [4, 256], replicated
- grad_conv_scan_bias: float32 [256], replicated
- grad_step_bias: float32 [48], P('tensor')
- grad_decay_log: float32 [48], P('tensor')
- grad_skip: float32 [48], P('tensor')
- grad_gate_gain: float32 [3072], P('tensor')
- grad_weight_out: float32 [3072, 1536], P('tensor')
All inputs are finite; a program needn't handle non-finite values.
Results may differ from a plain program's by a relative error of at most 0.0088.
Values sent between devices are 32-bit elements; how exact they have to be, the bound alone decides.
A program may use at most 192 MiB of HBM per device.

v0:
```python
import jax
import jax.numpy as jnp
from jax import lax
from jax.sharding import PartitionSpec as P

SPAN = 256
SEQ_LEN = 512
INNER = 3072


EPS = 1e-05
HIGHEST = lax.Precision.HIGHEST


def conv_silu(sequence, kernel, kernel_bias):
    kernel_width = kernel.shape[0]
    length = sequence.shape[1]
    padded = jnp.pad(sequence, ((0, 0), (kernel_width - 1, 0), (0, 0)))
    summed = jnp.zeros_like(sequence) + kernel_bias
    for offset in range(kernel_width):
        summed = summed + kernel[offset] * padded[:, offset : offset + length, :]
    return jax.nn.silu(summed)


def state_scan(head_input, step_size, rate, input_b, input_c, skip_gain):
    batch_size, length, head_count, head_width = head_input.shape
    block_count = length // SPAN
    state_dim = input_b.shape[-1]
    block_shape = (batch_size, block_count, SPAN)
    head_values = head_input.reshape(block_shape + (head_count, head_width))
    log_decay = (step_size * rate).reshape(block_shape + (head_count,))
    cumulative = jnp.cumsum(log_decay, axis=2)
    weighted = head_values * step_size.reshape(block_shape + (head_count,))[..., None]
    blocked_b = input_b.reshape(block_shape + (state_dim,))
    blocked_c = input_c.reshape(block_shape + (state_dim,))
    row_index = lax.broadcasted_iota(jnp.int32, (SPAN, SPAN), 0)
    col_index = lax.broadcasted_iota(jnp.int32, (SPAN, SPAN), 1)
    lower_mask = row_index >= col_index
    cum_heads = jnp.transpose(cumulative, (0, 1, 3, 2))
    decay_gaps = cum_heads[..., :, None] - cum_heads[..., None, :]
    decay_table = jnp.where(lower_mask, jnp.exp(jnp.where(lower_mask, decay_gaps, 0.0)), 0.0)
    intersection = jnp.einsum("bcin,bcjn->bcij", blocked_c, blocked_b, precision=HIGHEST)
    mix_table = decay_table * intersection[:, :, None]
    inner_part = jnp.einsum("bchij,bcjhp->bcihp", mix_table, weighted, precision=HIGHEST)
    span_total = cumulative[:, :, -1:, :]
    to_finish = jnp.exp(span_total - cumulative)
    span_states = jnp.einsum(
        "bcjn,bcjhp->bchpn", blocked_b, weighted * to_finish[..., None], precision=HIGHEST
    )
    span_decay = jnp.exp(span_total[:, :, 0, :])

    def carry_step(carried, pieces):
        piece_state, piece_decay = pieces
        return (carried * piece_decay[..., None, None] + piece_state, carried)

    initial = jnp.zeros((batch_size, head_count, head_width, state_dim), jnp.float32)
    final_state, entering = lax.scan(
        carry_step, initial, (jnp.moveaxis(span_states, 1, 0), jnp.moveaxis(span_decay, 1, 0))
    )
    entering = jnp.moveaxis(entering, 0, 1)
    outer_part = (
        jnp.einsum("bcin,bchpn->bcihp", blocked_c, entering, precision=HIGHEST)
        * jnp.exp(cumulative)[..., None]
    )
    result = inner_part + outer_part + skip_gain[:, None] * head_values
    return result.reshape(batch_size, length, head_count * head_width)


def mixer_path(
    value_branch,
    scan_act,
    step_branch,
    conv_value,
    conv_value_bias,
    step_bias,
    decay_log,
    skip_gain,
):
    value_act = conv_silu(value_branch, conv_value, conv_value_bias)
    step_size = jax.nn.softplus(step_branch + step_bias)
    head_count = step_bias.shape[0]
    head_input = value_act.reshape(value_act.shape[:2] + (head_count, -1))
    half_width = scan_act.shape[-1] // 2
    return state_scan(
        head_input,
        step_size,
        -jnp.exp(decay_log),
        scan_act[..., :half_width],
        scan_act[..., half_width:],
        skip_gain,
    )


def as_sequences(matrix, seq_count):
    return matrix.reshape(seq_count, -1, matrix.shape[-1])


def per_device(
    hidden_in,
    norm_gain,
    weight_gate,
    weight_value,
    weight_step,
    weight_scan,
    conv_value,
    conv_value_bias,
    conv_scan,
    conv_scan_bias,
    step_bias,
    decay_log,
    skip_gain,
    gate_gain,
    weight_out,
    cotangent,
):
    tokens_here = hidden_in.shape[0]
    seq_count = tokens_here // SEQ_LEN
    model_width = hidden_in.shape[1]
    share_width = model_width // lax.axis_size("tensor")
    first_col = lax.axis_index("tensor") * share_width
    inputs = hidden_in.astype(jnp.float32)
    inv_rms = lax.rsqrt(jnp.mean(inputs * inputs, axis=1) + EPS)
    unit_in = inputs * inv_rms[:, None]
    normed = (unit_in * norm_gain).astype(jnp.bfloat16)
    gate_branch = jnp.dot(normed, weight_gate, preferred_element_type=jnp.float32)
    value_branch = jnp.dot(normed, weight_value, preferred_element_type=jnp.float32)
    step_branch = jnp.dot(normed, weight_step, preferred_element_type=jnp.float32)
    scan_branch = jnp.dot(normed, weight_scan, preferred_element_type=jnp.float32)
    scan_act, scan_pullback = jax.vjp(
        conv_silu, as_sequences(scan_branch, seq_count), conv_scan, conv_scan_bias
    )
    ssd_out, ssd_pullback = jax.vjp(
        mixer_path,
        as_sequences(value_branch, seq_count),
        scan_act,
        as_sequences(step_branch, seq_count),
        conv_value,
        conv_value_bias,
        step_bias,
        decay_log,
        skip_gain,
    )
    ssd_flat = ssd_out.reshape(tokens_here, -1)
    gate_act = jax.nn.silu(gate_branch)
    gated = ssd_flat * gate_act
    squares = lax.psum(jnp.sum(gated * gated, axis=1), "tensor")
    inv_gate = lax.rsqrt(squares / INNER + EPS)
    unit_gate = gated * inv_gate[:, None]
    gate_normed = (unit_gate * gate_gain).astype(jnp.bfloat16)
    partial_out = jnp.dot(gate_normed, weight_out, preferred_element_type=jnp.float32)
    summed_out = lax.psum(partial_out, "tensor")
    mixed_share = lax.dynamic_slice_in_dim(summed_out, first_col, share_width, 1)
    block_out = lax.dynamic_slice_in_dim(inputs, first_col, share_width, 1) + mixed_share
    d_normed = jnp.einsum("td,kd->tk", cotangent, weight_out, preferred_element_type=jnp.float32)
    grad_weight_out = jnp.einsum(
        "tk,td->kd", gate_normed, cotangent, preferred_element_type=jnp.float32
    )
    grad_gate_gain = jnp.sum(d_normed * unit_gate, axis=0)
    d_unit = d_normed * gate_gain
    gate_dot = lax.psum(jnp.sum(d_unit * unit_gate, axis=1), "tensor")
    d_gated = inv_gate[:, None] * (d_unit - unit_gate * (gate_dot / INNER)[:, None])
    d_ssd = d_gated * gate_act
    sigmoid_gate = jax.nn.sigmoid(gate_branch)
    d_gate = d_gated * ssd_flat * sigmoid_gate * (1.0 + gate_branch * (1.0 - sigmoid_gate))
    (
        d_value,
        d_scan_part,
        d_step,
        grad_conv_value,
        grad_conv_value_bias,
        grad_step_bias,
        grad_decay_log,
        grad_skip,
    ) = ssd_pullback(d_ssd.reshape(ssd_out.shape))
    d_scan_act = lax.psum(d_scan_part, "tensor")
    d_scan, grad_conv_scan, grad_conv_scan_bias = scan_pullback(d_scan_act)
    gate_rounded = d_gate.astype(jnp.bfloat16)
    value_rounded = d_value.reshape(tokens_here, -1).astype(jnp.bfloat16)
    step_rounded = d_step.reshape(tokens_here, -1).astype(jnp.bfloat16)
    scan_rounded = d_scan.reshape(tokens_here, -1).astype(jnp.bfloat16)
    grad_weight_gate = jnp.einsum(
        "td,tk->dk", normed, gate_rounded, preferred_element_type=jnp.float32
    )
    grad_weight_value = jnp.einsum(
        "td,tk->dk", normed, value_rounded, preferred_element_type=jnp.float32
    )
    grad_weight_step = jnp.einsum(
        "td,tk->dk", normed, step_rounded, preferred_element_type=jnp.float32
    )
    grad_weight_scan = jnp.einsum(
        "td,tk->dk", normed, scan_rounded, preferred_element_type=jnp.float32
    )
    partial_in = (
        jnp.einsum("tk,dk->td", gate_rounded, weight_gate, preferred_element_type=jnp.float32)
        + jnp.einsum("tk,dk->td", value_rounded, weight_value, preferred_element_type=jnp.float32)
        + jnp.einsum("tk,dk->td", step_rounded, weight_step, preferred_element_type=jnp.float32)
    )
    unit_share = lax.dynamic_slice_in_dim(unit_in, first_col, share_width, 1)
    gain_share = lax.dynamic_slice_in_dim(norm_gain, first_col, share_width, 0)
    d_normed_in = lax.psum(partial_in, "tensor") + jnp.einsum(
        "tk,dk->td", scan_rounded, weight_scan, preferred_element_type=jnp.float32
    )
    in_dot = jnp.sum(d_normed_in * norm_gain * unit_in, axis=1)
    d_share = lax.dynamic_slice_in_dim(d_normed_in, first_col, share_width, 1)
    d_unit_share = d_share * gain_share
    grad_norm_gain = jnp.sum(d_share * unit_share, axis=0)
    upstream_share = lax.dynamic_slice_in_dim(cotangent, first_col, share_width, 1).astype(
        jnp.float32
    )
    grad_in = upstream_share + inv_rms[:, None] * (
        d_unit_share - unit_share * (in_dot / model_width)[:, None]
    )
    (
        grad_norm_gain,
        grad_weight_gate,
        grad_weight_value,
        grad_weight_step,
        grad_weight_scan,
        grad_conv_value,
        grad_conv_value_bias,
        grad_conv_scan,
        grad_conv_scan_bias,
        grad_step_bias,
        grad_decay_log,
        grad_skip,
        grad_gate_gain,
        grad_weight_out,
    ) = lax.psum(
        (
            grad_norm_gain,
            grad_weight_gate,
            grad_weight_value,
            grad_weight_step,
            grad_weight_scan,
            grad_conv_value,
            grad_conv_value_bias,
            grad_conv_scan,
            grad_conv_scan_bias,
            grad_step_bias,
            grad_decay_log,
            grad_skip,
            grad_gate_gain,
            grad_weight_out,
        ),
        "dp",
    )
    return (
        block_out,
        grad_in,
        grad_norm_gain,
        grad_weight_gate,
        grad_weight_value,
        grad_weight_step,
        grad_weight_scan,
        grad_conv_value,
        grad_conv_value_bias,
        grad_conv_scan,
        grad_conv_scan_bias,
        grad_step_bias,
        grad_decay_log,
        grad_skip,
        grad_gate_gain,
        grad_weight_out,
    )


def solution(mesh):
    placed = (
        P("dp", None),
        P(),
        P(None, "tensor"),
        P(None, "tensor"),
        P(None, "tensor"),
        P(),
        P(None, "tensor"),
        P("tensor"),
        P(),
        P(),
        P("tensor"),
        P("tensor"),
        P("tensor"),
        P("tensor"),
        P("tensor", None),
        P("dp", None),
    )
    return jax.shard_map(
        per_device,
        mesh=mesh,
        in_specs=placed,
        out_specs=(
            P("dp", "tensor"),
            P("dp", "tensor"),
            P("tensor"),
            P(None, "tensor"),
            P(None, "tensor"),
            P(None, "tensor"),
            P(),
            P(None, "tensor"),
            P("tensor"),
            P(),
            P(),
            P("tensor"),
            P("tensor"),
            P("tensor"),
            P("tensor"),
            P("tensor", None),
        ),
        check_vma=False,
    )
```

profile of v0, /device:TPU:1, one launch (start us, length us, event | category | flops | bytes accessed | tf_op | source)
XLA Modules:
  0.0 1002.7 jit_solution(8848355021561969164)
XLA Ops:
  10.4 2.6 compare_select_fusion.2
  14.7 5.0 fusion.109
  19.8 3.6 fusion.29
  23.4 5.4 reshape.608
  28.9 5.5 reshape.607
  41.3 6.2 copy.280
  47.5 6.1 copy.267
  53.6 6.0 fusion.68
  61.0 5.7 while.34
  67.3 4.5 fusion.52
  73.6 17.0 %fusion.24 = f32[1,2,256,24,64]{2,4,3,1,0:T(8,128)} fusion(f32[1,2,256,24,64]{2,4,3,1,0:T(8,128)} %copy.280, f32[2,256,24,64]{1,3,2,0:T(8,128)S(1)} %fusion.52, f32[24]{0:T(128)S(1)} %copy-done.73, f32[2,256,24]{1,2,0:T(8,128)S(1)} %copy.278, f32[2,256,256]{2,1,0:T(8,128)S(1)} %fusion.118, f32[2,24,256]{2,1,0:T(8,128)S(1)} %reduce_window_sum.50, ...), kind=kOutput, calls=%fused_computation.43 | convolution fusion | flops 2432434176 | bytes 13320288 | tf_op jit(solution)/shard_map/jvp(bchij,bcjhp->bcihp)/dot_general | solution.py:44
  90.5 5.8 copy.322
  96.4 6.3 reshape.609
  102.7 8.5 multiply_reduce_fusion.10
  111.2 4.5 psum.133
  115.7 7.7 fusion.103
  123.4 7.4 multiply_reduce_fusion.1
  130.8 3.9 psum.135
  134.7 9.3 fusion.25
  144.1 3.5 copy.284
  147.6 5.2 reshape_reshape.6
  152.8 5.2 reshape_reshape.5
  157.9 4.3 multiply_reduce_fusion.7
  162.2 5.8 fusion.71
  168.0 4.0 fusion.67
  175.0 6.5 while.35
  182.0 22.0 %fusion.10 = (f32[2,24,256]{2,1,0:T(8,128)S(1)}, f32[2,24,256]{2,1,0:T(8,128)S(1)}, f32[2,256,256]{2,1,0:T(8,128)}) fusion(f32[2,256,256]{2,1,0:T(8,128)} %copy-done.28, f32[2,24,256]{2,1,0:T(8,128)} %copy-done.46, pred[256,256]{1,0:T(8,128)(4,1)} %iota_compare_fusion, f32[2,256,24,64]{1,3,2,0:T(8,128)} %copy.267, f32[2,256,24]{1,2,0:T(8,128)S(1)} %bitcast.266, ...), kind=kOutput, calls=%fused_computation.20 | convolution fusion | flops 2451152896 | bytes 7602176 | tf_op jit(solution)/shard_map/transpose(jvp(bchij,bcjhp->bcihp))/dot_general | solution.py:44
  205.8 2.8 fusion.49
  208.6 14.9 %fusion.26 = (f32[2,256,24]{1,2,0:T(8,128)S(1)}, f32[2,256,24]{1,2,0:T(8,128)}, f32[1,2,256,24,64]{2,4,3,1,0:T(8,128)}) fusion(f32[2,24,64,256]{3,2,1,0:T(8,128)S(1)} %fusion.49, f32[1,2,256,24,64]{2,4,3,1,0:T(8,128)} %copy.280, f32[2,256,24]{1,2,0:T(8,128)S(1)} %bitcast.267, f32[1,2,256,24,64]{2,1,4,3,0:T(2,128)S(1)} %copy-done.21, f32[24]{0:T(128)S(1)} %copy-done.74, ...), kind=kOutput, calls=%fused_computation.48 | convolution fusion | flops 2436341760 | bytes 16564320 | tf_op jit(solution)/shard_map/transpose(jvp(bchij,bcjhp->bcihp))/dot_general | solution.py:44
  228.6 5.2 reduce-window.16
  236.3 5.6 fusion.79
  245.4 7.1 fusion.119
  252.5 5.8 copy.324
  258.3 6.2 reshape.610
  264.5 9.1 multiply_reduce_fusion.4
  278.0 5.1 convolution_add_fusion.2
  283.4 2.3 convolution_add_fusion
  288.3 7.1 fusion.106
  295.4 5.3 fusion.105
  300.8 5.3 fusion.102
  306.0 148.0 %all-reduce.29.cloned.1.call-done = (f32[512,1536]{1,0:T(8,128)}, f32[512,1536]{1,0:T(8,128)}, f32[1,512,256]{2,1,0:T(8,128)}) async-done(((f32[512,1536]{1,0:T(8,128)}, f32[512,1536]{1,0:T(8,128)}, f32[1,512,256]{2,1,0:T(8,128)}), (f32[512,1536]{1,0:T(8,128)}, f32[512,1536]{1,0:T(8,128)}, f32[1,512,256]{2,1,0:T(8,128)})) %all-reduce.29.cloned.1.call-update) | async-done | bytes 6815760 | tf_op jit(solution)/shard_map/psum | solution.py:151
  460.4 3.0 multiply_reduce_fusion.6
  465.1 60.5 %all-reduce.21 = (f32[768]{0:T(1024)}, f32[4,1536]{1,0:T(4,128)}, f32[1536]{0:T(1024)}, f32[4,256]{1,0:T(4,128)}, f32[256]{0:T(256)}, /*index=5*/f32[24]{0:T(128)}, f32[24]{0:T(128)}, f32[24]{0:T(128)}, f32[1536]{0:T(1024)}) all-reduce(f32[768]{0:T(1024)S(1)} %get-tuple-element.412, ...), channel_id=1, replica_groups=mesh['dp'=16,'tensor'=2] {'dp'}, use_global_device_ids=true, to_apply=%region_26.27 | all-reduce | flops 11336 | bytes 90688 | tf_op jit(solution)/shard_map/psum | solution.py:228
  525.6 3.5 dynamic-slice_add_fusion
  529.1 443.8 %all-reduce.27.cloned.1.call-done = (f32[1536,1536]{1,0:T(8,128)}, f32[1536,1536]{1,0:T(8,128)}, f32[1536,24]{0,1:T(8,128)}, f32[1536,256]{1,0:T(8,128)}, f32[1536,1536]{1,0:T(8,128)}) async-done(((f32[1536,1536]{1,0:T(8,128)}, f32[1536,1536]{1,0:T(8,128)}, f32[1536,24]{0,1:T(8,128)}, f32[1536,256]{1,0:T(8,128)}, f32[1536,1536]{1,0:T(8,128)}), (f32[1536,1536]{1,0:T(8,128)}, f32[1536,1536]{1,0:T(8,128)}, ...) | async-done | bytes 30031888 | tf_op jit(solution)/shard_map/psum | solution.py:228
  972.9 8.5 copy.393
  981.4 8.4 copy.394
  991.6 3.7 copy.397
  (268 shorter events, 59.8 us)
Async XLA Ops:
  7.2 30.1 %copy-start = (bf16[1536,256]{1,0:T(8,128)(2,1)S(1)}, bf16[1536,256]{1,0:T(8,128)(2,1)}, u32[]{:S(2)}) copy-start(bf16[1536,256]{1,0:T(8,128)(2,1)} %param.25) | copy-start | bytes 2359300
  7.2 7.5 copy-start.54
  7.2 7.4 copy-start.51
  7.2 446.9 %all-reduce.29.cloned.1.call-start = ((), (), s32[]{:S(2)}) async-start(), calls=%async_computation.1 | async-start | bytes 13631488 | tf_op jit(solution)/shard_map/psum | solution.py:151
  8.6 11.2 %copy-start.71 = (f32[24]{0:T(128)}, f32[24]{0:T(128)S(1)}, u32[]{:S(2)}) copy-start(f32[24]{0:T(128)S(1)} %exponential_negate_fusion) | copy-start | bytes 292
  10.4 26.9 %copy-start.52 = (f32[512]{0:T(512)}, f32[512]{0:T(512)S(1)}, u32[]{:S(2)}) copy-start(f32[512]{0:T(512)S(1)} %add_rsqrt_fusion.1) | copy-start | bytes 6148
  28.9 5.5 copy-start.67
  41.3 26.0 %copy-start.13 = (f32[1,512,128]{2,1,0:T(8,128)}, f32[1,512,128]{2,1,0:T(8,128)S(1)}, u32[]{:S(2)}) copy-start(f32[1,512,128]{2,1,0:T(8,128)S(1)} %get-tuple-element.426) | copy-start | bytes 786436
  53.6 7.3 copy-start.69
  61.0 5.7 copy-start.29
  61.0 5.7 copy-start.30
  66.7 6.9 copy-start.4
  66.7 6.9 copy-start.43
  66.7 6.9 copy-start.73
  66.7 23.8 %copy-start.46 = (f32[2,24,256]{2,1,0:T(8,128)}, f32[2,24,256]{2,1,0:T(8,128)S(1)}, u32[]{:S(2)}) copy-start(f32[2,24,256]{2,1,0:T(8,128)S(1)} %reduce_window_sum.50) | copy-start | bytes 147460
  67.3 23.2 %copy-start.28 = (f32[2,256,256]{2,1,0:T(8,128)}, f32[2,256,256]{2,1,0:T(8,128)S(1)}, u32[]{:S(2)}) copy-start(f32[2,256,256]{2,1,0:T(8,128)S(1)} %fusion.118) | copy-start | bytes 1572868
  96.4 6.3 copy-start.5
  115.6 7.7 copy-start.49
  115.6 7.7 copy-start.8
  115.6 7.7 copy-start.18
  115.6 7.7 copy-start.32
  162.2 5.8 copy-start.14
  182.0 23.7 %copy-start.7 = (f32[2,1,24,64,128]{4,3,2,1,0:T(8,128)S(1)}, f32[2,1,24,64,128]{4,3,2,1,0:T(8,128)}, u32[]{:S(2)}) copy-start(f32[2,1,24,64,128]{4,3,2,1,0:T(8,128)} %get-tuple-element.193) | copy-start | bytes 4718596
  208.6 15.1 %copy-start.17 = (f32[1,2,24,256]{2,1,3,0:T(2,128)S(1)}, f32[1,2,24,256]{2,1,3,0:T(2,128)}, u32[]{:S(2)}) copy-start(f32[1,2,24,256]{2,1,3,0:T(2,128)} %copy-done.16) | copy-start | bytes 147460
  223.5 11.0 %copy-start.15 = (f32[1,512,128]{2,1,0:T(8,128)S(1)}, f32[1,512,128]{2,1,0:T(8,128)}, u32[]{:S(2)}) copy-start(f32[1,512,128]{2,1,0:T(8,128)} %copy-done.13) | copy-start | bytes 786436
  236.2 6.7 copy-start.23
  236.2 6.7 copy-start.27
  264.5 9.2 copy-start.36
  264.5 9.2 copy-start.38
  264.5 9.2 copy-start.40
  264.5 9.2 copy-start.42
  264.5 13.4 %slice-start.3 = ((s8[4718592]{0:T(1024)(128)(4,1)}), s8[4194304]{0:T(1024)(128)(4,1)S(1)}, s32[]{:S(2)}) async-start(s8[4718592]{0:T(1024)(128)(4,1)} %bitcast.294), calls=%async_computation.5 | async-start | bytes 8388608
  278.0 5.4 copy-start.34
  285.7 687.2 %all-reduce.27.cloned.1.call-start = ((), (), s32[]{:S(2)}) async-start(), calls=%async_computation | async-start | bytes 60063744 | tf_op jit(solution)/shard_map/psum | solution.py:228
  288.3 7.1 copy-start.25
  295.4 5.3 copy-start.19
  295.4 5.3 copy-start.33
  300.7 153.4 %copy-start.12 = (f32[512,256]{1,0:T(8,128)S(1)}, f32[512,256]{1,0:T(8,128)}, u32[]{:S(2)}) copy-start(f32[512,256]{1,0:T(8,128)} %copy-done.11) | copy-start | bytes 1572868
  300.7 153.4 %copy-start.22 = (f32[1,512,256]{2,1,0:T(8,128)S(1)}, f32[1,512,256]{2,1,0:T(8,128)}, u32[]{:S(2)}) copy-start(f32[1,512,256]{2,1,0:T(8,128)} %get-tuple-element.406) | copy-start | bytes 1572868
  300.7 154.8 %copy-start.58 = (f32[1,256]{1,0:T(1,128)S(1)}, f32[1,256]{1,0:T(1,128)}, u32[]{:S(2)}) copy-start(f32[1,256]{1,0:T(1,128)} %copy-done.57) | copy-start | bytes 3076
  300.7 154.8 %copy-start.60 = (f32[1,256]{1,0:T(1,128)S(1)}, f32[1,256]{1,0:T(1,128)}, u32[]{:S(2)}) copy-start(f32[1,256]{1,0:T(1,128)} %copy-done.59) | copy-start | bytes 3076
  300.8 154.8 %copy-start.62 = (f32[1,256]{1,0:T(1,128)S(1)}, f32[1,256]{1,0:T(1,128)}, u32[]{:S(2)}) copy-start(f32[1,256]{1,0:T(1,128)} %copy-done.61) | copy-start | bytes 3076
  300.8 154.8 %copy-start.64 = (f32[1,256]{1,0:T(1,128)S(1)}, f32[1,256]{1,0:T(1,128)}, u32[]{:S(2)}) copy-start(f32[1,256]{1,0:T(1,128)} %copy-done.63) | copy-start | bytes 3076
  972.9 18.7 %slice-start = ((s8[9437184]{0:T(1024)(128)(4,1)}), s8[4194304]{0:T(1024)(128)(4,1)S(1)}, s32[]{:S(2)}) async-start(s8[9437184]{0:T(1024)(128)(4,1)} %bitcast.244), calls=%async_computation.2 | async-start | bytes 8388608
  972.9 18.7 %slice-start.1 = ((s8[9437184]{0:T(1024)(128)(4,1)}), s8[4194304]{0:T(1024)(128)(4,1)S(1)}, s32[]{:S(2)}) async-start(s8[9437184]{0:T(1024)(128)(4,1)} %bitcast.244), calls=%async_computation.3 | async-start | bytes 8388608
  981.4 8.4 copy-start.31
  981.4 9.1 copy-start.26
  981.4 10.2 %slice-start.2 = ((s8[9437184]{0:T(1024)(128)(4,1)}), s8[1048576]{0:T(1024)(128)(4,1)S(1)}, s32[]{:S(2)}) async-start(s8[9437184]{0:T(1024)(128)(4,1)} %bitcast.244), calls=%async_computation.4 | async-start | bytes 2097152
  (35 other events, 134.3 us)
Sparse Core Ops, SparseCore 0:
  285.8 168.2 all-reduce.28
  460.5 512.3 all-reduce.26
where the time goes:
time: 1010 us; the launch traced here: 1000 us
  waiting for transfers between devices  592 us (59%)
  matrix products  157 us (16%)
  local copies, waits for them, and re-layouts  104 us (10%)
  blocking collectives  68.8 us (7%)
  other arithmetic  64.8 us (6%)
  between operations  15.7 us (2%)
    psum x1, waiting for transfers between devices, per_device(): lax.psum((grad_norm_gain, grad_weight_gate, grad_weight_value, grad_weigh...  444 us
    psum x1, waiting for transfers between devices, per_device(): summed_out = lax.psum(partial_out, 'tensor')  148 us
    psum x1, blocking collectives, per_device(): lax.psum((grad_norm_gain, grad_weight_gate, grad_weight_value, grad_weigh...  60.5 us
    dot_general x3, matrix products, state_scan(): jnp.einsum('bchij,bcjhp->bcihp', mix_table, weighted, precision=HIGHEST)  54 us
    unnamed x168, local copies, waits for them, and re-layouts  27.1 us
    reshape x4, local copies, waits for them, and re-layouts, state_scan(): head_values = head_input.reshape(block_shape + (head_count, head_width))  23.2 us
  transfers between devices with their start and end apart: 2, of which 2 were waited for; matrix products, arithmetic and copies ran while one was open for 3% of the time, Pallas kernels for 0%

commit v1 on v0

--- a/solution.py
+++ b/solution.py
@@ -1,11 +1,356 @@
+import functools
+
 import jax
 import jax.numpy as jnp
 from jax import lax
+from jax.experimental import pallas as pl
+from jax.experimental.pallas import tpu as pltpu
 from jax.sharding import PartitionSpec as P
 
 SPAN = 256
 SEQ_LEN = 512
 INNER = 3072
+
+MESH = pl.DeviceIdType.MESH
+GROUP = 32
+TREES = 4
+
+
+def grid_dims(dp_size):
+    chips = dp_size // 2
+    if chips == 8:
+        return (4, 2)
+    if chips == 32:
+        return (2, 4, 4)
+    return (chips,)
+
+
+def build_trees(dims):
+    count = 1
+    for size in dims:
+        count *= size
+
+    def coords(node):
+        out = []
+        for size in reversed(dims):
+            out.append(node % size)
+            node //= size
+        return tuple(reversed(out))
+
+    def index(place):
+        node = 0
+        for size, at in zip(dims, place):
+            node = node * size + at
+        return node
+
+    rank = len(dims)
+    plans = []
+    for tree in range(TREES):
+        order = [(axis + 1 + tree // 2) % rank for axis in range(rank)]
+        root = [
+            (size - 1) // 2 if (tree % 2 == 0) else size // 2 for size in dims
+        ]
+        parent, children = [-1] * count, [[] for _ in range(count)]
+        for node in range(count):
+            place = list(coords(node))
+            for axis in order:
+                if place[axis] != root[axis]:
+                    place[axis] += 1 if place[axis] < root[axis] else -1
+                    parent[node] = index(place)
+                    break
+        for node in range(count):
+            if parent[node] >= 0:
+                children[parent[node]].append(node)
+
+        def height(node):
+            return max([0] + [1 + height(child) for child in children[node]])
+
+        def depth(node):
+            return 0 if parent[node] < 0 else 1 + depth(parent[node])
+
+        plans.append(
+            dict(
+                parent=parent,
+                children=children,
+                slot=[
+                    children[parent[node]].index(node) if parent[node] >= 0 else 0
+                    for node in range(count)
+                ],
+                height=[height(node) for node in range(count)],
+                depth=[depth(node) for node in range(count)],
+                top=height(index(root)),
+            )
+        )
+    return plans
+
+
+def pick(me, table):
+    value = jnp.int32(table[0])
+    for at in range(1, len(table)):
+        if table[at] != table[0] or True:
+            value = jnp.where(me == at, jnp.int32(table[at]), value)
+    return value
+
+
+def all_reduce_kernel(
+    plans, splits, hop, part, out, own_buf, sib_buf, up_buf, acc,
+    own_sem, sib_send, sib_recv, up_send, up_recv, dn_send, dn_recv,
+    tail_send, tail_recv, local_sem,
+):
+    depth_slots = own_buf.shape[0]
+    width = own_buf.shape[2]
+    rows = part.shape[0]
+    chunks = rows // (2 * GROUP) * splits
+    me = lax.axis_index("dp")
+    core = lax.rem(me, 2)
+    chip = me // 2
+    sibling = me + 1 - 2 * core
+    kids = up_buf.shape[1]
+    first = 1
+    node = []
+    for plan in plans:
+        parent = pick(chip, plan["parent"])
+        node.append(
+            dict(
+                root=parent < 0,
+                parent=parent * 2 + core,
+                slot=pick(chip, plan["slot"]),
+                kids=pick(chip, [len(c) for c in plan["children"]]),
+                child=[
+                    pick(chip, [c[i] if i < len(c) else 0 for c in plan["children"]]) * 2 + core
+                    for i in range(kids)
+                ],
+                up=first + hop * pick(chip, plan["height"]),
+                down=first + hop * (plan["top"] + pick(chip, plan["depth"])),
+            )
+        )
+    last = first + hop * max(p["top"] + max(p["depth"]) for p in plans) + hop
+
+    count = len(plans[0]["parent"])
+    links = []
+    for at in range(count):
+        near = set()
+        for plan in plans:
+            if plan["parent"][at] >= 0:
+                near.add(plan["parent"][at])
+            near.update(plan["children"][at])
+        links.append(sorted(near))
+    most = max(len(near) for near in links)
+    barrier = pltpu.get_barrier_semaphore()
+    pl.semaphore_signal(barrier, inc=1, device_id={"dp": sibling}, device_id_type=MESH)
+    degree = pick(chip, [len(near) for near in links])
+    for at in range(most):
+        other = pick(chip, [near[at] if at < len(near) else 0 for near in links]) * 2 + core
+
+        @pl.when(at < degree)
+        def _():
+            pl.semaphore_signal(barrier, inc=1, device_id={"dp": other}, device_id_type=MESH)
+
+    pl.semaphore_wait(barrier, degree + 1)
+
+    def place(chunk, side, tree=None):
+        row = (2 * (chunk // splits) + side) * GROUP
+        height = GROUP
+        if tree is not None:
+            row = row + tree * (GROUP // TREES)
+            height = GROUP // TREES
+        col = lax.rem(chunk, splits) * width
+        return pl.ds(pl.multiple_of(row, 8), height), pl.ds(pl.multiple_of(col, 128), width)
+
+    def slot_of(chunk):
+        return lax.rem(chunk, depth_slots)
+
+    def own_copy(chunk):
+        at = slot_of(chunk)
+        return pltpu.make_async_copy(part.at[place(chunk, core)], own_buf.at[at], own_sem.at[at])
+
+    def sib_copy(chunk):
+        at = slot_of(chunk)
+        return pltpu.make_async_remote_copy(
+            part.at[place(chunk, 1 - core)], sib_buf.at[at], sib_send.at[at], sib_recv.at[at],
+            device_id={"dp": sibling}, device_id_type=MESH,
+        )
+
+    def up_copy(tree, chunk):
+        at = slot_of(chunk)
+        return pltpu.make_async_remote_copy(
+            acc.at[tree, at], up_buf.at[tree, node[tree]["slot"], at],
+            up_send.at[tree, at], up_recv.at[tree, node[tree]["slot"], at],
+            device_id={"dp": node[tree]["parent"]}, device_id_type=MESH,
+        )
+
+    def up_arrival(tree, kid, chunk):
+        at = slot_of(chunk)
+        return pltpu.make_async_remote_copy(
+            acc.at[tree, at], up_buf.at[tree, kid, at],
+            up_send.at[tree, at], up_recv.at[tree, kid, at],
+            device_id={"dp": node[tree]["child"][kid]}, device_id_type=MESH,
+        )
+
+    def down_copy(tree, kid, chunk, at_root):
+        at = slot_of(chunk)
+        here = place(chunk, core, tree)
+        return pltpu.make_async_remote_copy(
+            acc.at[tree, at] if at_root else out.at[here], out.at[here],
+            dn_send.at[tree, kid, at], dn_recv.at[tree, at],
+            device_id={"dp": node[tree]["child"][kid]}, device_id_type=MESH,
+        )
+
+    def tail_copy(tree, chunk, at_root, side):
+        at = slot_of(chunk)
+        here = place(chunk, side, tree)
+        return pltpu.make_async_remote_copy(
+            acc.at[tree, at] if at_root else out.at[here], out.at[here],
+            tail_send.at[tree, at], tail_recv.at[tree, at],
+            device_id={"dp": sibling}, device_id_type=MESH,
+        )
+
+    def local_copy(tree, chunk):
+        at = slot_of(chunk)
+        return pltpu.make_async_copy(
+            acc.at[tree, at], out.at[place(chunk, core, tree)], local_sem.at[tree, at]
+        )
+
+    def finish_sends(tree, chunk):
+        info = node[tree]
+
+        @pl.when(info["root"])
+        def _():
+            local_copy(tree, chunk).wait()
+
+        @pl.when(jnp.logical_not(info["root"]))
+        def _():
+            up_copy(tree, chunk).wait_send()
+
+        for kid in range(kids):
+            @pl.when(kid < info["kids"])
+            def _():
+                down_copy(tree, kid, chunk, False).wait_send()
+
+        tail_copy(tree, chunk, False, core).wait_send()
+
+    def step(tick, _):
+        for tree in range(TREES):
+            chunk = tick - (node[tree]["down"] + hop)
+
+            @pl.when((chunk >= 0) & (chunk < chunks))
+            def _():
+                tail_copy(tree, chunk, False, 1 - core).wait_recv()
+
+        @pl.when(tick < chunks)
+        def _():
+            @pl.when(tick >= depth_slots)
+            def _():
+                sib_copy(tick - depth_slots).wait_send()
+
+            own_copy(tick).start()
+            sib_copy(tick).start()
+
+        ready = tick - first
+
+        @pl.when((ready >= 0) & (ready < chunks))
+        def _():
+            own_copy(ready).wait()
+            sib_copy(ready).wait_recv()
+
+        for tree in range(TREES):
+            info = node[tree]
+            chunk = tick - info["up"]
+            rows_here = slice(tree * (GROUP // TREES), (tree + 1) * (GROUP // TREES))
+
+            @pl.when((chunk >= 0) & (chunk < chunks))
+            def _():
+                at = slot_of(chunk)
+
+                @pl.when(chunk >= depth_slots)
+                def _():
+                    finish_sends(tree, chunk - depth_slots)
+
+                acc[tree, at] = own_buf[at, rows_here, :] + sib_buf[at, rows_here, :]
+                for kid in range(kids):
+                    @pl.when(kid < info["kids"])
+                    def _():
+                        up_arrival(tree, kid, chunk).wait_recv()
+                        acc[tree, at] = acc[tree, at] + up_buf[tree, kid, at]
+
+        for tree in range(TREES):
+            info = node[tree]
+            chunk = tick - info["up"]
+            live = (chunk >= 0) & (chunk < chunks)
+
+            @pl.when(live & jnp.logical_not(info["root"]))
+            def _():
+                up_copy(tree, chunk).start()
+
+            @pl.when(live & info["root"])
+            def _():
+                for kid in range(kids):
+                    @pl.when(kid < info["kids"])
+                    def _():
+                        down_copy(tree, kid, chunk, True).start()
+                tail_copy(tree, chunk, True, core).start()
+                local_copy(tree, chunk).start()
+
+        for tree in range(TREES):
+            info = node[tree]
+            chunk = tick - info["down"]
+
+            @pl.when((chunk >= 0) & (chunk < chunks) & jnp.logical_not(info["root"]))
+            def _():
+                down_copy(tree, 0, chunk, False).wait_recv()
+                for kid in range(kids):
+                    @pl.when(kid < info["kids"])
+                    def _():
+                        down_copy(tree, kid, chunk, False).start()
+                tail_copy(tree, chunk, False, core).start()
+
+        return 0
+
+    lax.fori_loop(0, chunks + last, step, 0)
+
+    def drain(at, _):
+        chunk = chunks - depth_slots + at
+
+        @pl.when(chunk >= 0)
+        def _():
+            sib_copy(chunk).wait_send()
+            for tree in range(TREES):
+                finish_sends(tree, chunk)
+
+        return 0
+
+    lax.fori_loop(0, depth_slots, drain, 0)
+
+
+def tree_all_reduce(part, splits=1, hop=2):
+    dp_size = lax.axis_size("dp")
+    plans = build_trees(grid_dims(dp_size))
+    kids = max(max(len(c) for c in p["children"]) for p in plans)
+    reach = max(p["top"] + max(p["depth"]) for p in plans)
+    slots = 1 + hop * (reach + 1) + 2
+    rows, cols = part.shape
+    width = cols // splits
+    dma = pltpu.SemaphoreType.DMA
+    small = GROUP // TREES
+    return pl.pallas_call(
+        functools.partial(all_reduce_kernel, plans, splits, hop),
+        out_shape=jax.ShapeDtypeStruct((rows, cols), jnp.float32),
+        in_specs=[pl.BlockSpec(memory_space=pl.ANY)],
+        out_specs=pl.BlockSpec(memory_space=pl.ANY),
+        scratch_shapes=[
+            pltpu.VMEM((slots, GROUP, width), jnp.float32),
+            pltpu.VMEM((slots, GROUP, width), jnp.float32),
+            pltpu.VMEM((TREES, kids, slots, small, width), jnp.float32),
+            pltpu.VMEM((TREES, slots, small, width), jnp.float32),
+            dma((slots,)), dma((slots,)), dma((slots,)),
+            dma((TREES, slots)), dma((TREES, kids, slots)),
+            dma((TREES, kids, slots)), dma((TREES, slots)),
+            dma((TREES, slots)), dma((TREES, slots)), dma((TREES, slots)),
+        ],
+        compiler_params=pltpu.CompilerParams(
+            collective_id=0, has_side_effects=True, vmem_limit_bytes=60 << 20
+        ),
+    )(part)
 
 
 EPS = 1e-05
@@ -210,40 +555,54 @@
     grad_in = upstream_share + inv_rms[:, None] * (
         d_unit_share - unit_share * (in_dot / model_width)[:, None]
     )
-    (
-        grad_norm_gain,
-        grad_weight_gate,
-        grad_weight_value,
-        grad_weight_step,
-        grad_weight_scan,
-        grad_conv_value,
-        grad_conv_value_bias,
-        grad_conv_scan,
-        grad_conv_scan_bias,
-        grad_step_bias,
-        grad_decay_log,
-        grad_skip,
-        grad_gate_gain,
-        grad_weight_out,
-    ) = lax.psum(
-        (
-            grad_norm_gain,
+    wide = grad_weight_gate.shape[1]
+    share = grad_norm_gain.shape[0]
+    heads = grad_skip.shape[0]
+    tail = jnp.concatenate(
+        [grad_norm_gain, grad_step_bias, grad_decay_log, grad_skip, grad_conv_scan_bias]
+    )
+    small = jnp.concatenate(
+        [
+            grad_weight_step.T,
+            grad_conv_value,
+            grad_conv_value_bias[None],
+            grad_gate_gain[None],
+            jnp.pad(tail, (0, model_width - tail.shape[0]))[None],
+            jnp.pad(grad_conv_scan.reshape(-1), (0, model_width - grad_conv_scan.size))[None],
+        ]
+    )
+    scan_wide = grad_weight_scan.shape[1]
+    rows = 3 * model_width + scan_wide + small.shape[0]
+    spare = -rows % (2 * GROUP)
+    packed = jnp.concatenate(
+        [
+            grad_weight_out,
             grad_weight_gate,
             grad_weight_value,
-            grad_weight_step,
-            grad_weight_scan,
-            grad_conv_value,
-            grad_conv_value_bias,
-            grad_conv_scan,
-            grad_conv_scan_bias,
-            grad_step_bias,
-            grad_decay_log,
-            grad_skip,
-            grad_gate_gain,
-            grad_weight_out,
-        ),
-        "dp",
-    )
+            grad_weight_scan.T,
+            small,
+            jnp.zeros((spare, model_width), jnp.float32),
+        ]
+    )
+    summed = tree_all_reduce(packed)
+    grad_weight_out = summed[:wide]
+    grad_weight_gate = summed[wide : wide + model_width]
+    grad_weight_value = summed[wide + model_width : wide + 2 * model_width]
+    at = wide + 2 * model_width
+    grad_weight_scan = summed[at : at + scan_wide].T
+    at += scan_wide
+    grad_weight_step = summed[at : at + heads].T
+    at += heads
+    grad_conv_value = summed[at : at + 4]
+    grad_conv_value_bias = summed[at + 4]
+    grad_gate_gain = summed[at + 5]
+    line = summed[at + 6]
+    grad_norm_gain = line[:share]
+    grad_step_bias = line[share : share + heads]
+    grad_decay_log = line[share + heads : share + 2 * heads]
+    grad_skip = line[share + 2 * heads : share + 3 * heads]
+    grad_conv_scan_bias = line[share + 3 * heads : share + 3 * heads + scan_wide]
+    grad_conv_scan = summed[at + 7][: 4 * scan_wide].reshape(4, scan_wide)
     return (
         block_out,
         grad_in,

time: 1010 us -> 870 us (0.86)
  waiting for transfers between devices: 592 us -> 143 us
  Pallas kernels: 0 us -> 283 us
  local copies, waits for them, and re-layouts: 104 us -> 188 us
  blocking collectives: 68.8 us -> 8.34 us
    psum x1 -> x0, waiting for transfers between devices: 444 us -> none  [per_device(): lax.psum((grad_norm_gain, grad_weight_gate, grad_weight_value, grad_weigh...]
    pallas_call x0 -> x1, Pallas kernels: none -> 283 us  [tree_all_reduce(): pl.pallas_call(functools.partial(all_reduce_kernel, plans, splits, hop),...]
    concatenate x0 -> x2, local copies, waits for them, and re-layouts: none -> 69.6 us  [the longest x1 69.5 us: per_device(): jnp.concatenate([grad_weight_out, grad_weight_gate, grad_weight_value, gr...]
    psum x1 -> x0, blocking collectives: 60.5 us -> none  [per_device(): lax.psum((grad_norm_gain, grad_weight_gate, grad_weight_value, grad_weigh...]
    slice x1 -> x8, local copies, waits for them, and re-layouts: 0.17 us -> 27.7 us  [the longest x1 19.8 us: per_device(): grad_weight_out = summed[:wide]]
    unnamed x168 -> x175, local copies, waits for them, and re-layouts: 27.1 us -> 8.55 us
  transfers between devices with their start and end apart: 2 -> 1, of which waited for: 2 -> 1; matrix products, arithmetic and copies ran while one was open for 3% -> 3% of each run, Pallas kernels for 0% -> 0%
where the time goes in v1:
time: 870 us; the launch traced here: 858 us
  Pallas kernels  283 us (33%)
  local copies, waits for them, and re-layouts  188 us (22%)
  matrix products  154 us (18%)
  waiting for transfers between devices  143 us (16%)
  other arithmetic  65.7 us (8%)
  between operations  15.4 us (2%)
    pallas_call x1, Pallas kernels, tree_all_reduce(): pl.pallas_call(functools.partial(all_reduce_kernel, plans, splits, hop),...  283 us
    psum x1, waiting for transfers between devices, per_device(): summed_out = lax.psum(partial_out, 'tensor')  143 us
    concatenate x1, local copies, waits for them, and re-layouts, per_device(): jnp.concatenate([grad_weight_out, grad_weight_gate, grad_weight_value, gr...  69.5 us
    dot_general x3, matrix products, state_scan(): jnp.einsum('bchij,bcjhp->bcihp', mix_table, weighted, precision=HIGHEST)  54 us
    reshape x4, local copies, waits for them, and re-layouts, state_scan(): head_values = head_input.reshape(block_shape + (head_count, head_width))  23.2 us
    slice x1, local copies, waits for them, and re-layouts, per_device(): grad_weight_out = summed[:wide]  19.8 us
  transfers between devices with their start and end apart: 1, of which 1 were waited for; matrix products, arithmetic and copies ran while one was open for 3% of the time, Pallas kernels for 0%

profile of v1, /device:TPU:1, one launch (start us, length us, event | category | flops | bytes accessed | tf_op | source)
XLA Modules:
  0.0 858.3 jit_solution(18381392998772114249)
XLA Ops:
  10.4 2.6 compare_select_fusion.2
  14.7 5.0 fusion.109
  19.8 3.6 fusion.29
  23.4 5.4 reshape.624
  28.9 5.5 reshape.623
  41.3 6.2 copy.286
  47.5 6.1 copy.273
  53.6 6.0 fusion.68
  61.0 5.7 while.34
  67.4 4.5 fusion.52
  73.6 17.0 %fusion.24 = f32[1,2,256,24,64]{2,4,3,1,0:T(8,128)} fusion(f32[1,2,256,24,64]{2,4,3,1,0:T(8,128)} %copy.286, f32[2,256,24,64]{1,3,2,0:T(8,128)S(1)} %fusion.52, f32[24]{0:T(128)S(1)} %copy-done.81, f32[2,256,24]{1,2,0:T(8,128)S(1)} %copy.284, f32[2,256,256]{2,1,0:T(8,128)S(1)} %fusion.119, f32[2,24,256]{2,1,0:T(8,128)S(1)} %reduce_window_sum.50, ...), kind=kOutput, calls=%fused_computation.43 | convolution fusion | flops 2432434176 | bytes 13320288 | tf_op jit(solution)/shard_map/jvp(bchij,bcjhp->bcihp)/dot_general | solution.py:389
  90.6 5.8 copy.329
  96.4 6.3 reshape.625
  102.7 8.5 multiply_reduce_fusion.10
  111.2 4.4 psum.35
  115.7 7.7 fusion.103
  123.4 7.4 multiply_reduce_fusion.1
  130.9 3.9 psum.37
  134.8 9.5 %fusion.25 = (f32[1536]{0:T(1024)}, f32[512,1536]{1,0:T(8,128)}, bf16[512,1536]{1,0:T(8,128)(2,1)}) fusion(f32[1,512,1536]{2,1,0:T(8,128)} %get-tuple-element.508, f32[512,1536]{1,0:T(8,128)} %get-tuple-element.543, f32[512]{0:T(512)S(1)} %broadcast_multiply_fusion.10, f32[512,1536]{1,0:T(8,128)} %get-tuple-element.502, f32[512,1536]{1,0:T(8,128)} %get-tuple-element.544, ...), kind=kLoop, calls=%fused_computation.45 | loop fusion | flops 18086400 | bytes 20463616 | tf_op jit(solution)/shard_map/transpose(jvp())/reduce_sum | solution.py:410
  144.3 3.5 copy.290
  147.8 5.2 reshape_reshape.6
  153.0 5.2 reshape_reshape.5
  158.2 4.3 multiply_reduce_fusion.7
  162.4 5.8 fusion.71
  168.2 4.0 fusion.67
  175.2 6.2 while.35
  182.0 22.1 %fusion.10 = (f32[2,24,256]{2,1,0:T(8,128)S(1)}, f32[2,24,256]{2,1,0:T(8,128)S(1)}, f32[2,256,256]{2,1,0:T(8,128)}) fusion(f32[2,256,256]{2,1,0:T(8,128)} %copy-done.31, f32[2,24,256]{2,1,0:T(8,128)} %copy-done.49, pred[256,256]{1,0:T(8,128)(4,1)} %iota_compare_fusion, f32[2,256,24,64]{1,3,2,0:T(8,128)} %copy.273, f32[2,256,24]{1,2,0:T(8,128)S(1)} %bitcast.278, ...), kind=kOutput, calls=%fused_computation.20 | convolution fusion | flops 2451152896 | bytes 7602176 | tf_op jit(solution)/shard_map/transpose(jvp(bchij,bcjhp->bcihp))/dot_general | solution.py:389
  205.8 2.8 fusion.49
  208.6 14.9 %fusion.26 = (f32[2,256,24]{1,2,0:T(8,128)S(1)}, f32[2,256,24]{1,2,0:T(8,128)}, f32[1,2,256,24,64]{2,4,3,1,0:T(8,128)}) fusion(f32[2,24,64,256]{3,2,1,0:T(8,128)S(1)} %fusion.49, f32[1,2,256,24,64]{2,4,3,1,0:T(8,128)} %copy.286, f32[2,256,24]{1,2,0:T(8,128)S(1)} %bitcast.279, f32[1,2,256,24,64]{2,1,4,3,0:T(2,128)S(1)} %copy-done.22, f32[24]{0:T(128)S(1)} %copy-done.82, ...), kind=kOutput, calls=%fused_computation.48 | convolution fusion | flops 2436341760 | bytes 16564320 | tf_op jit(solution)/shard_map/transpose(jvp(bchij,bcjhp->bcihp))/dot_general | solution.py:389
  225.4 2.2 bitcast_add_fusion.6
  228.7 5.2 reduce-window.16
  236.3 5.6 fusion.79
  245.4 7.1 fusion.120
  252.6 5.8 copy.331
  258.4 6.2 reshape.626
  264.6 9.2 %multiply_reduce_fusion.4 = (f32[1536]{0:T(1024)S(1)}, f32[1536]{0:T(1024)S(1)}, f32[1536]{0:T(1024)S(1)}, f32[1536]{0:T(1024)S(1)}, f32[1536]{0:T(1024)S(1)}, /*index=5*/f32[1,512,1536]{2,1,0:T(8,128)S(1)}) fusion(f32[1,512,1536]{2,1,0:T(8,128)} %bitcast.257, f32[512,1536]{1,0:T(8,128)} %copy-done.1, f32[1,512,1536]{2,1,0:T(8,128)} %get-tuple-element.508, ...), kind=kLoop, calls=%fused_computation.55 | loop fusion | flops 14148096 | bytes 15759360 | tf_op jit(solution)/shard_map/transpose(jvp())/reduce_sum | solution.py:366
  278.2 5.1 convolution_add_fusion.2
  284.0 2.3 convolution_add_fusion
  287.7 2.1 convert_element_type.34
  294.1 6.8 fusion.106
  300.9 5.3 fusion.105
  306.2 5.4 fusion.102
  311.7 143.0 %all-reduce.26.cloned.1.call-done = (f32[512,1536]{1,0:T(8,128)}, f32[512,1536]{1,0:T(8,128)}, f32[1,512,256]{2,1,0:T(8,128)}) async-done(((f32[512,1536]{1,0:T(8,128)}, f32[512,1536]{1,0:T(8,128)}, f32[1,512,256]{2,1,0:T(8,128)}), (f32[512,1536]{1,0:T(8,128)}, f32[512,1536]{1,0:T(8,128)}, f32[1,512,256]{2,1,0:T(8,128)})) %all-reduce.26.cloned.1.call-update) | async-done | bytes 6815760 | tf_op jit(solution)/shard_map/psum | solution.py:496
  454.7 2.0 multiply_reduce_fusion.15
  463.1 2.4 multiply_reduce_fusion.12
  465.7 69.5 %concatenate.7.part = f32[4928,1536]{1,0:T(8,128)} concatenate(f32[1536,1536]{1,0:T(8,128)} %fusion.102, f32[1536,1536]{1,0:T(8,128)} %fusion.106, f32[1536,1536]{1,0:T(8,128)} %fusion.105, f32[256,1536]{1,0:T(8,128)S(1)} %copy-done.28, f32[24,1536]{1,0:T(8,128)S(1)} %fusion.97, f32[4,1536]{1,0:T(4,128)S(1)} %copy-done.34, f32[1,1536]{1,0:T(1,128)S(1)} %copy-done.55, ...), dimensions={0} | concatenate | bytes 60555264 | tf_op jit(solution)/shard_map/concatenate | solution.py:577
  535.3 283.2 %shard_map.279 = f32[4928,1536]{1,0:T(8,128)} custom-call(f32[4928,1536]{1,0:T(8,128)} %concatenate.7.part), custom_call_target="tpu_custom_call" | custom-call | tf_op jit(solution)/shard_map/pallas_call | solution.py:335
  829.3 19.8 %fusion.116 = (f32[1536,1536]{1,0:T(8,128)}, f32[1536,1536]{1,0:T(8,128)}, f32[1536,1536]{1,0:T(8,128)}) fusion(f32[4928,1536]{1,0:T(8,128)} %shard_map.279), kind=kLoop, calls=%fused_computation.201 | loop fusion | bytes 56623104 | tf_op jit(solution)/shard_map/slice | solution.py:588
  (289 shorter events, 70.8 us)
Async XLA Ops:
  7.2 30.1 %copy-start = (bf16[1536,256]{1,0:T(8,128)(2,1)S(1)}, bf16[1536,256]{1,0:T(8,128)(2,1)}, u32[]{:S(2)}) copy-start(bf16[1536,256]{1,0:T(8,128)(2,1)} %param.25) | copy-start | bytes 2359300
  7.2 7.5 copy-start.57
  7.2 7.4 copy-start.56
  7.2 447.5 %all-reduce.26.cloned.1.call-start = ((), (), s32[]{:S(2)}) async-start(), calls=%async_computation | async-start | bytes 13631488 | tf_op jit(solution)/shard_map/psum | solution.py:496
  8.6 11.2 %copy-start.78 = (f32[24]{0:T(128)}, f32[24]{0:T(128)S(1)}, u32[]{:S(2)}) copy-start(f32[24]{0:T(128)S(1)} %exponential_negate_fusion) | copy-start | bytes 292
  10.4 26.9 %copy-start.60 = (f32[512]{0:T(512)}, f32[512]{0:T(512)S(1)}, u32[]{:S(2)}) copy-start(f32[512]{0:T(512)S(1)} %add_rsqrt_fusion.1) | copy-start | bytes 6148
  14.7 5.1 copy-start.38
  14.7 5.1 copy-start.40
  14.7 5.1 copy-start.42
  28.9 5.5 copy-start.72
  41.3 26.1 %copy-start.14 = (f32[1,512,128]{2,1,0:T(8,128)}, f32[1,512,128]{2,1,0:T(8,128)S(1)}, u32[]{:S(2)}) copy-start(f32[1,512,128]{2,1,0:T(8,128)S(1)} %get-tuple-element.532) | copy-start | bytes 786436
  53.6 7.3 copy-start.76
  61.0 5.7 copy-start.32
  61.0 5.7 copy-start.33
  66.7 6.9 copy-start.4
  66.7 6.9 copy-start.46
  66.7 6.9 copy-start.81
  66.8 23.8 %copy-start.49 = (f32[2,24,256]{2,1,0:T(8,128)}, f32[2,24,256]{2,1,0:T(8,128)S(1)}, u32[]{:S(2)}) copy-start(f32[2,24,256]{2,1,0:T(8,128)S(1)} %reduce_window_sum.50) | copy-start | bytes 147460
  67.4 23.2 %copy-start.31 = (f32[2,256,256]{2,1,0:T(8,128)}, f32[2,256,256]{2,1,0:T(8,128)S(1)}, u32[]{:S(2)}) copy-start(f32[2,256,256]{2,1,0:T(8,128)S(1)} %fusion.119) | copy-start | bytes 1572868
  96.4 6.3 copy-start.5
  115.7 7.7 copy-start.52
  115.7 7.7 copy-start.8
  115.7 7.7 copy-start.19
  115.7 7.7 copy-start.35
  162.4 5.8 copy-start.15
  182.0 23.8 %copy-start.7 = (f32[2,1,24,64,128]{4,3,2,1,0:T(8,128)S(1)}, f32[2,1,24,64,128]{4,3,2,1,0:T(8,128)}, u32[]{:S(2)}) copy-start(f32[2,1,24,64,128]{4,3,2,1,0:T(8,128)} %get-tuple-element.193) | copy-start | bytes 4718596
  208.6 15.1 %copy-start.18 = (f32[1,2,24,256]{2,1,3,0:T(2,128)S(1)}, f32[1,2,24,256]{2,1,3,0:T(2,128)}, u32[]{:S(2)}) copy-start(f32[1,2,24,256]{2,1,3,0:T(2,128)} %copy-done.17) | copy-start | bytes 147460
  223.5 11.0 %copy-start.16 = (f32[1,512,128]{2,1,0:T(8,128)S(1)}, f32[1,512,128]{2,1,0:T(8,128)}, u32[]{:S(2)}) copy-start(f32[1,512,128]{2,1,0:T(8,128)} %copy-done.14) | copy-start | bytes 786436
  236.3 6.7 copy-start.25
  236.3 6.7 copy-start.29
  264.6 9.2 %copy-start.39 = (f32[1536]{0:T(1024)S(1)}, f32[1536]{0:T(1024)}, u32[]{:S(2)}) copy-start(f32[1536]{0:T(1024)} %copy-done.38) | copy-start | bytes 18436
  264.6 9.3 %copy-start.41 = (f32[1536]{0:T(1024)S(1)}, f32[1536]{0:T(1024)}, u32[]{:S(2)}) copy-start(f32[1536]{0:T(1024)} %copy-done.40) | copy-start | bytes 18436
  264.6 9.3 %copy-start.43 = (f32[1536]{0:T(1024)S(1)}, f32[1536]{0:T(1024)}, u32[]{:S(2)}) copy-start(f32[1536]{0:T(1024)} %copy-done.42) | copy-start | bytes 18436
  264.6 9.3 %copy-start.45 = (f32[1536]{0:T(1024)S(1)}, f32[1536]{0:T(1024)}, u32[]{:S(2)}) copy-start(f32[1536]{0:T(1024)} %copy-done.44) | copy-start | bytes 18436
  264.6 13.5 %slice-start = ((s8[4718592]{0:T(1024)(128)(4,1)}), s8[4194304]{0:T(1024)(128)(4,1)S(1)}, s32[]{:S(2)}) async-start(s8[4718592]{0:T(1024)(128)(4,1)} %bitcast.308), calls=%async_computation.1 | async-start | bytes 8388608
  278.1 5.2 copy-start.26
  278.1 5.2 copy-start.48
  278.2 5.2 copy-start.79
  278.2 5.9 copy-start.37
  286.4 6.0 copy-start.83
  286.4 7.2 copy-start.61
  294.1 6.8 copy-start.27
  300.9 5.3 copy-start.9
  300.9 5.3 copy-start.20
  300.9 5.3 copy-start.36
  300.9 5.3 copy-start.53
  306.2 148.5 %copy-start.12 = (f32[512,256]{1,0:T(8,128)S(1)}, f32[512,256]{1,0:T(8,128)}, u32[]{:S(2)}) copy-start(f32[512,256]{1,0:T(8,128)} %copy-done.11) | copy-start | bytes 1572868
  306.2 148.5 %copy-start.24 = (f32[1,512,256]{2,1,0:T(8,128)S(1)}, f32[1,512,256]{2,1,0:T(8,128)}, u32[]{:S(2)}) copy-start(f32[1,512,256]{2,1,0:T(8,128)} %get-tuple-element.506) | copy-start | bytes 1572868
  (39 other events, 128.4 us)
Sparse Core Ops, SparseCore 0:
  286.5 168.2 all-reduce.25
